TPU v7x, 32 devices: a whole 2x2x4 slice. The times are simulated.
32 devices in a mesh: dp: 4 (over z), expert: 4 (over y, x), tensor: 2 (over core).
Axes of the slice: x: 2, y: 2, z: 4, core: 2. Of those that a mesh axis runs over, the one named last changes fastest.
Arguments:
- tokens: bfloat16 [512, 6144], P('dp', 'tensor'), may hold values from -6 to 6
- out_grad: bfloat16 [512, 6144], P('dp', 'tensor'), may hold values from -6 to 6
- router_weight: bfloat16 [6144, 4], P('tensor'), may hold values from -0.078125 to 0.078125
- gate_weight: bfloat16 [4, 6144, 8192], P('expert', 'tensor', 'dp'), may hold values from -0.078125 to 0.078125
- up_weight: bfloat16 [4, 6144, 8192], P('expert', 'tensor', 'dp'), may hold values from -0.078125 to 0.078125
- down_weight: bfloat16 [4, 8192, 6144], P('expert', 'dp', 'tensor'), may hold values from -0.0625 to 0.0625
- expert_index: int32 [512, 2], P('dp'), may hold values from 0 to 3, as said below
- slot_index: int32 [512, 2], P('dp'), may hold values from 0 to 95, as said below
Outputs:
- tokens_grad: bfloat16 [512, 6144], P(('dp', 'expert'), 'tensor')
- router_grad: float32 [6144, 4], P('tensor')
- gate_grad: bfloat16 [4, 6144, 8192], P('expert', 'tensor', 'dp')
- up_grad: bfloat16 [4, 6144, 8192], P('expert', 'tensor', 'dp')
- down_grad: bfloat16 [4, 8192, 6144], P('expert', 'dp', 'tensor')
Inputs may be any that keep to these rules, and one draw needn't show every extreme that they name: `expert_index`: each row names two different experts; in each aligned block of 128 rows no expert is named more than 96 times, and one expert is named exactly 96 times in every block. `slot_index`: entry k of a row is a slot of the expert in entry k of the same row of expert_index; within one aligned block of 128 rows the choices of one expert have distinct slots.
All inputs are finite; a program needn't handle non-finite values.
Results may differ from a plain program's by a relative error of at most 0.025.
Values may be sent and summed in bfloat16 or wider, within the bound.
A program may use at most 128 MiB of HBM per device.

v0:
```python
import jax
import jax.numpy as jnp
from jax import lax
from jax.sharding import PartitionSpec as P

CAP = 96
highest = lax.Precision.HIGHEST


def contract_rows(left_side, right_side):
    return lax.dot_general(
        left_side, right_side, (((0,), (0,)), ((), ())), preferred_element_type=jnp.float32
    )


def contract_cols(left_side, right_side):
    return lax.dot_general(
        left_side, right_side, (((1,), (1,)), ((), ())), preferred_element_type=jnp.float32
    )


def split_parts(values):
    high_part = values.astype(jnp.bfloat16)
    low_part = (values - high_part.astype(jnp.float32)).astype(jnp.bfloat16)
    return (high_part, low_part)


def table_apply(form, table_low, values):
    high_part, low_part = split_parts(values)
    return jnp.einsum(form, table_low, high_part, preferred_element_type=jnp.float32) + jnp.einsum(
        form, table_low, low_part, preferred_element_type=jnp.float32
    )


def slot_table(experts_here, slots_here, expert_id, capacity):
    positions = lax.broadcasted_iota(jnp.int32, (capacity, experts_here.shape[0]), 0)
    first_table = (experts_here[:, 0] == expert_id)[None, :] & (
        slots_here[:, 0][None, :] == positions
    )
    second_table = (experts_here[:, 1] == expert_id)[None, :] & (
        slots_here[:, 1][None, :] == positions
    )
    return (first_table.astype(jnp.float32), second_table.astype(jnp.float32))


def hidden_terms(gate_sum, up_sum, grad_act, slot_prob):
    gate_sigmoid = jax.nn.sigmoid(gate_sum)
    hidden = (gate_sum * gate_sigmoid * up_sum).astype(jnp.bfloat16)
    prob_grad = jnp.sum(hidden.astype(jnp.float32) * grad_act, axis=1)
    act_grad = slot_prob.astype(jnp.float32)[:, None] * grad_act
    grad_gate = (act_grad * up_sum * gate_sigmoid * (1.0 + gate_sum * (1.0 - gate_sigmoid))).astype(
        jnp.bfloat16
    )
    grad_up = (act_grad * gate_sum * gate_sigmoid).astype(jnp.bfloat16)
    return (hidden, grad_gate, grad_up, prob_grad)


def shards(
    tokens, out_grad, router_weight, gate_weight, up_weight, down_weight, expert_index, slot_index
):
    capacity = CAP
    expert_count = router_weight.shape[1]
    expert_id = lax.axis_index("expert")
    logits = lax.psum(jnp.dot(tokens, router_weight, preferred_element_type=jnp.float32), "tensor")
    chosen = jnp.take_along_axis(logits, expert_index, axis=1)
    pick_prob = jnp.stack(
        [jax.nn.sigmoid(chosen[:, 0] - chosen[:, 1]), jax.nn.sigmoid(chosen[:, 1] - chosen[:, 0])],
        axis=1,
    )
    prob_wide = pick_prob.astype(jnp.bfloat16).astype(jnp.float32)
    first_table, second_table = slot_table(expert_index, slot_index, expert_id, capacity)
    select = first_table + second_table
    select_low = select.astype(jnp.bfloat16)
    local_tokens = jnp.dot(select_low, tokens, preferred_element_type=jnp.float32).astype(
        jnp.bfloat16
    )
    local_grads = jnp.dot(select_low, out_grad, preferred_element_type=jnp.float32).astype(
        jnp.bfloat16
    )
    local_prob = (
        jnp.dot(first_table, prob_wide[:, 0], precision=highest)
        + jnp.dot(second_table, prob_wide[:, 1], precision=highest)
    ).astype(jnp.bfloat16)
    slot_tokens, slot_grads, slot_prob = (
        lax.all_gather(local_tokens, "dp", axis=0, tiled=True),
        lax.all_gather(local_grads, "dp", axis=0, tiled=True),
        lax.all_gather(local_prob, "dp", axis=0, tiled=True),
    )
    gate_block = gate_weight[0]
    up_block = up_weight[0]
    down_block = down_weight[0]
    gate_part = jnp.dot(slot_tokens, gate_block, preferred_element_type=jnp.float32)
    up_part = jnp.dot(slot_tokens, up_block, preferred_element_type=jnp.float32)
    grad_part = contract_cols(slot_grads, down_block)
    gate_sum, up_sum, grad_sum = (
        lax.psum(gate_part.astype(jnp.bfloat16), "tensor").astype(jnp.float32),
        lax.psum(up_part.astype(jnp.bfloat16), "tensor").astype(jnp.float32),
        lax.psum(grad_part.astype(jnp.bfloat16), "tensor").astype(jnp.float32),
    )
    hidden, grad_gate, grad_up, prob_grad = hidden_terms(gate_sum, up_sum, grad_sum, slot_prob)
    scaled_grads = (slot_prob.astype(jnp.float32)[:, None] * slot_grads.astype(jnp.float32)).astype(
        jnp.bfloat16
    )
    down_grad = contract_rows(hidden, scaled_grads).astype(jnp.bfloat16)
    gate_grad = contract_rows(slot_tokens, grad_gate).astype(jnp.bfloat16)
    up_grad = contract_rows(slot_tokens, grad_up).astype(jnp.bfloat16)
    slot_dx = contract_cols(grad_gate, gate_block) + contract_cols(grad_up, up_block)
    own_expert = (lax.broadcasted_iota(jnp.int32, (1, expert_count), 1) == expert_id).astype(
        jnp.float32
    )
    row_dx, row_prob = (
        lax.psum_scatter(
            slot_dx.astype(jnp.bfloat16), "dp", scatter_dimension=0, tiled=True
        ).astype(jnp.float32),
        lax.psum_scatter(
            prob_grad.astype(jnp.bfloat16), "dp", scatter_dimension=0, tiled=True
        ).astype(jnp.float32),
    )
    token_dx = table_apply("cn,cd->nd", select_low, row_dx)
    token_prob = table_apply("cn,c->n", select_low, row_prob)
    token_term, prob_rows = (
        lax.psum_scatter(
            token_dx.astype(jnp.bfloat16), "expert", scatter_dimension=0, tiled=True
        ).astype(jnp.float32),
        lax.psum_scatter(
            (token_prob[:, None] * own_expert).astype(jnp.bfloat16),
            "expert",
            scatter_dimension=0,
            tiled=True,
        ).astype(jnp.float32),
    )
    quarter = token_term.shape[0]
    offset = expert_id * quarter
    part_prob = lax.dynamic_slice_in_dim(pick_prob, offset, quarter, 0)
    part_experts = lax.dynamic_slice_in_dim(expert_index, offset, quarter, 0)
    part_tokens = lax.dynamic_slice_in_dim(tokens, offset, quarter, 0)
    pick_grad = jnp.take_along_axis(prob_rows, part_experts, axis=1)
    mixed_grad = jnp.sum(part_prob * pick_grad, axis=1, keepdims=True)
    weights = part_prob * (pick_grad - mixed_grad)
    onehot = (
        part_experts[:, :, None] == lax.broadcasted_iota(jnp.int32, (1, 1, expert_count), 2)
    ).astype(jnp.float32)
    logit_grad = jnp.sum(onehot * weights[:, :, None], axis=1)
    router_rows = router_weight.astype(jnp.float32)
    tokens_grad = (token_term + jnp.dot(logit_grad, router_rows.T, precision=highest)).astype(
        jnp.bfloat16
    )
    router_part = jnp.dot(part_tokens.astype(jnp.float32).T, logit_grad, precision=highest)
    router_grad = lax.psum(router_part, ("dp", "expert"))
    return (tokens_grad, router_grad, gate_grad[None], up_grad[None], down_grad[None])


def solution(mesh):
    in_specs = (
        P("dp", "tensor"),
        P("dp", "tensor"),
        P("tensor", None),
        P("expert", "tensor", "dp"),
        P("expert", "tensor", "dp"),
        P("expert", "dp", "tensor"),
        P("dp", None),
        P("dp", None),
    )
    out_specs = (
        P(("dp", "expert"), "tensor"),
        P("tensor", None),
        P("expert", "tensor", "dp"),
        P("expert", "tensor", "dp"),
        P("expert", "dp", "tensor"),
    )
    return jax.shard_map(shards, mesh=mesh, in_specs=in_specs, out_specs=out_specs, check_vma=False)
```

profile of v0, /device:TPU:0, one launch (start us, length us, event | category | flops | bytes accessed | tf_op | source)
XLA Modules:
  0.0 356.0 jit_solution(7405413484927864889)
XLA Ops:
  7.2 0.8 slice_bitcast_fusion.1
  8.0 0.8 compare_bitcast_fusion.1
  8.8 1.1 convolution_convert_fusion
  10.0 2.3 convolution_convert_fusion.1
  12.3 50.6 %all-gather.5.cloned.1.call-done = bf16[384,3072]{1,0:T(8,128)(2,1)} async-done(((bf16[96,3072]{1,0:T(8,128)(2,1)}), bf16[384,3072]{1,0:T(8,128)(2,1)}) %all-gather.5.cloned.1.call-update) | async-done | bytes 2359312 | tf_op jit(solution)/shard_map/all_gather | solution.py:85
  62.9 11.3 %fusion.31 = bf16[384,2048]{1,0:T(8,128)(2,1)} fusion(bf16[384,3072]{1,0:T(8,128)(2,1)} %all-gather.5.cloned.1.call-done, bf16[1,3072,2048]{2,1,0:T(8,128)(2,1)} %param.11), kind=kOutput, calls=%fused_computation.44 | convolution fusion | flops 4832624640 | bytes 16515072 | tf_op jit(solution)/shard_map/dot_general | solution.py:92
  74.1 9.4 %fusion.28 = bf16[384,2048]{1,0:T(8,128)(2,1)} fusion(bf16[384,3072]{1,0:T(8,128)(2,1)S(1)} %copy-done.8, bf16[1,3072,2048]{2,1,0:T(8,128)(2,1)} %param.12), kind=kOutput, calls=%fused_computation.43 | convolution fusion | flops 4832624640 | bytes 16515072 | tf_op jit(solution)/shard_map/dot_general | solution.py:93
  83.5 30.3 %all-gather.3.cloned.1.call-done = bf16[384,3072]{1,0:T(8,128)(2,1)} async-done(((bf16[96,3072]{1,0:T(8,128)(2,1)}), bf16[384,3072]{1,0:T(8,128)(2,1)}) %all-gather.3.cloned.1.call-update) | async-done | bytes 2359312 | tf_op jit(solution)/shard_map/all_gather | solution.py:86
  113.8 9.6 %fusion.25 = bf16[384,2048]{1,0:T(8,128)(2,1)} fusion(bf16[384,3072]{1,0:T(8,128)(2,1)} %all-gather.3.cloned.1.call-done, bf16[1,2048,3072]{2,1,0:T(8,128)(2,1)} %param.13), kind=kOutput, calls=%fused_computation.42 | convolution fusion | flops 4832624640 | bytes 16515072 | tf_op jit(solution)/shard_map/dot_general | solution.py:17
  123.5 0.6 copy-done.6
  124.1 0.1 copy.59
  124.2 0.1 reshape.58
  124.4 0.3 fusion.66
  124.7 2.5 psum.35
  127.2 2.4 gather_fusion
  129.5 0.1 reshape.61
  129.7 0.6 fusion.65
  131.1 0.1 convolution_bitcast_fusion.3
  131.2 0.1 fusion.37
  131.3 0.2 dynamic-update-slice
  131.5 20.0 %all-reduce.6.cloned.1.call-done = (bf16[384,2048]{1,0:T(8,128)(2,1)}, bf16[384,2048]{1,0:T(8,128)(2,1)}, bf16[384,2048]{1,0:T(8,128)(2,1)}) async-done(((bf16[384,2048]{1,0:T(8,128)(2,1)}, bf16[384,2048]{1,0:T(8,128)(2,1)}, bf16[384,2048]{1,0:T(8,128)(2,1)}), (bf16[384,2048]{1,0:T(8,128)(2,1)}, bf16[384,2048]{1,0:T(8,128)(2,1)}, bf16[384,2048]{1,0:T(8,128)(2,1)})) %all-reduce.6.cloned.1.call-update) | async-done | bytes 4718608 | tf_op jit(solution)/shard_map/psum | solution.py:98
  151.5 3.7 %fusion.14 = bf16[384]{0:T(512)(128)(2,1)S(1)} fusion(bf16[384,2048]{1,0:T(8,128)(2,1)} %get-tuple-element.7, bf16[384,2048]{1,0:T(8,128)(2,1)} %get-tuple-element.8, bf16[384,2048]{1,0:T(8,128)(2,1)} %get-tuple-element.9), kind=kLoop, calls=%fused_computation.31 | loop fusion | flops 9436800 | bytes 4719360 | tf_op jit(solution)/shard_map/reduce_sum | solution.py:49
  155.2 12.1 %all-reduce.2 = (bf16[384]{0:T(512)(128)(2,1)S(1)}, bf16[384]{0:T(512)(128)(2,1)S(1)}) all-reduce(bf16[384]{0:T(512)(128)(2,1)S(1)} %fusion.14, bf16[384]{0:T(512)(128)(2,1)S(1)} %dynamic-update-slice), channel_id=4, replica_groups=mesh['dp'=4,'expert'=4,'tensor'=2] {'dp'}, use_global_device_ids=true, to_apply=%region_7.8.clone | all-reduce | flops 768 | bytes 3072
  167.4 12.2 %fusion = f32[384,3072]{1,0:T(8,128)} fusion(bf16[1,3072,2048]{2,1,0:T(8,128)(2,1)} %param.11, bf16[384,2048]{1,0:T(8,128)(2,1)S(1)} %copy-done.1, bf16[384,2048]{1,0:T(8,128)(2,1)} %get-tuple-element.7, bf16[384,2048]{1,0:T(8,128)(2,1)} %get-tuple-element.9, f32[384]{0:T(512)S(1)} %convert_element_type.124), kind=kOutput, calls=%fused_computation.2 | convolution fusion | flops 4842848256 | bytes 22021632 | tf_op jit(solution)/shard_map/dot_general | solution.py:17
  179.6 16.1 %add_convert_fusion = bf16[384,3072]{1,0:T(8,128)(2,1)} fusion(f32[384,3072]{1,0:T(8,128)} %fusion, bf16[1,3072,2048]{2,1,0:T(8,128)(2,1)} %param.12, bf16[384,2048]{1,0:T(8,128)(2,1)S(1)} %copy-done.2, bf16[384,2048]{1,0:T(8,128)(2,1)} %get-tuple-element.7, f32[384]{0:T(512)S(1)} %convert_element_type.124), kind=kOutput, calls=%fused_computation.20 | convolution fusion | flops 4841275392 | bytes 22808064 | tf_op jit(solution)/shard_map/dot_general | solution.py:17
  195.8 0.1 bitcast_or_fusion
  195.9 0.1 copy.61
  196.0 0.1 reshape.64
  196.8 0.2 convolution_bitcast_fusion.1
  197.0 0.2 fusion.35
  197.2 0.7 copy.63
  198.0 0.3 reduce-scatter.8.cloned.1.call-start
  198.3 13.5 %convert_bitcast_fusion.2 = bf16[1,3072,2048]{2,1,0:T(8,128)(2,1)} fusion(bf16[384,3072]{1,0:T(8,128)(2,1)} %all-gather.5.cloned.1.call-done, bf16[384,2048]{1,0:T(8,128)(2,1)S(1)} %copy-done.1, bf16[384,2048]{1,0:T(8,128)(2,1)} %get-tuple-element.7, bf16[384,2048]{1,0:T(8,128)(2,1)} %get-tuple-element.9, f32[384]{0:T(512)S(1)} %convert_element_type.124), kind=kOutput, calls=%fused_computation.14 | convolution fusion | flops 4849139712 | bytes 19662336 | tf_op jit(solution)/shard_map/dot_general | solution.py:11
  211.8 10.3 %convert_bitcast_fusion.1 = bf16[1,3072,2048]{2,1,0:T(8,128)(2,1)} fusion(bf16[384,3072]{1,0:T(8,128)(2,1)S(1)} %copy-done.9, bf16[384,2048]{1,0:T(8,128)(2,1)S(1)} %copy-done.3, bf16[384,2048]{1,0:T(8,128)(2,1)S(1)} %copy-done.4, f32[384]{0:T(512)S(1)} %convert_element_type.124), kind=kOutput, calls=%fused_computation.13 | convolution fusion | flops 4845207552 | bytes 18089472 | tf_op jit(solution)/shard_map/dot_general | solution.py:11
  222.1 19.6 %reduce-scatter.6.cloned.1.call-done = bf16[96,3072]{1,0:T(8,128)(2,1)} async-done(((bf16[384,3072]{1,0:T(8,128)(2,1)}), bf16[96,3072]{1,0:T(8,128)(2,1)}) %reduce-scatter.6.cloned.1.call-update) | async-done | bytes 589840 | tf_op jit(solution)/shard_map/reduce_scatter | solution.py:112
  241.8 1.5 fusion.48
  243.2 2.4 fusion.12
  245.6 12.1 %convert_bitcast_fusion = bf16[1,2048,3072]{2,1,0:T(8,128)(2,1)} fusion(bf16[384,3072]{1,0:T(8,128)(2,1)} %all-gather.3.cloned.1.call-done, f32[384]{0:T(512)S(1)} %convert_element_type.124, bf16[384,2048]{1,0:T(8,128)(2,1)S(1)} %copy-done.1, bf16[384,2048]{1,0:T(8,128)(2,1)} %get-tuple-element.9), kind=kOutput, calls=%fused_computation.12 | convolution fusion | flops 4847960064 | bytes 18089472 | tf_op jit(solution)/shard_map/dot_general | solution.py:11
  257.7 10.6 %reduce-scatter.10.cloned.1.call-done = bf16[32,4]{1,0:T(8,128)(2,1)} async-done(((bf16[128,4]{1,0:T(8,128)(2,1)}), bf16[32,4]{1,0:T(8,128)(2,1)}) %reduce-scatter.10.cloned.1.call-update) | async-done | bytes 272
  268.4 0.8 copy.64
  269.2 0.9 gather_fusion.1
  270.0 0.1 reshape.67
  270.1 0.1 copy.62
  270.2 0.1 multiply_reduce_fusion
  270.3 0.1 subtract_multiply_fusion
  270.4 0.2 fusion.38
  270.6 76.5 %psum.39 = f32[3072,4]{0,1:T(4,128)} all-reduce(f32[3072,4]{0,1:T(4,128)S(1)} %fusion.38), channel_id=1, replica_groups=mesh['dp'=4,'expert'=4,'tensor'=2] {'dp','expert'}, use_global_device_ids=true, to_apply=%region_11.12 | all-reduce | flops 12288 | bytes 98304 | tf_op jit(solution)/shard_map/psum | solution.py:149
  347.1 2.0 fusion.13
  (43 shorter events, 0.6 us)
Async XLA Ops:
  7.2 1.6 copy-start
  7.2 55.7 %all-gather.5.cloned.1.call-start = ((), (), s32[]{:S(2)}) async-start(), calls=%async_computation.4 | async-start | bytes 2949120 | tf_op jit(solution)/shard_map/all_gather | solution.py:85
  9.9 103.9 %all-gather.3.cloned.1.call-start = ((), (), s32[]{:S(2)}) async-start(), calls=%async_computation.3 | async-start | bytes 2949120 | tf_op jit(solution)/shard_map/all_gather | solution.py:86
  12.3 139.3 %all-reduce.6.cloned.1.call-start = ((), (), s32[]{:S(2)}) async-start(), calls=%async_computation.8 | async-start | bytes 9437184 | tf_op jit(solution)/shard_map/psum | solution.py:98
  62.9 11.3 %copy-start.8 = (bf16[384,3072]{1,0:T(8,128)(2,1)S(1)}, bf16[384,3072]{1,0:T(8,128)(2,1)}, u32[]{:S(2)}) copy-start(bf16[384,3072]{1,0:T(8,128)(2,1)} %all-gather.5.cloned.1.call-done) | copy-start | bytes 7077892
  123.4 0.7 copy-start.6
  123.4 0.9 copy-start.5
  123.5 118.3 %reduce-scatter.6.cloned.1.call-start = ((), (), s32[]{:S(2)}) async-start(), calls=%async_computation.5 | async-start | bytes 2949120 | tf_op jit(solution)/shard_map/reduce_scatter | solution.py:112
  127.2 2.6 copy-start.7
  151.5 15.8 %copy-start.1 = (bf16[384,2048]{1,0:T(8,128)(2,1)S(1)}, bf16[384,2048]{1,0:T(8,128)(2,1)}, u32[]{:S(2)}) copy-start(bf16[384,2048]{1,0:T(8,128)(2,1)} %get-tuple-element.8) | copy-start | bytes 4718596
  167.4 12.2 %copy-start.2 = (bf16[384,2048]{1,0:T(8,128)(2,1)S(1)}, bf16[384,2048]{1,0:T(8,128)(2,1)}, u32[]{:S(2)}) copy-start(bf16[384,2048]{1,0:T(8,128)(2,1)} %get-tuple-element.9) | copy-start | bytes 4718596
  195.7 72.6 %reduce-scatter.10.cloned.1.call-start = ((), (), s32[]{:S(2)}) async-start(), calls=%async_computation.7 | async-start | bytes 40960
  198.0 149.2 %reduce-scatter.8.cloned.1.call-start = ((), (), s32[]{:S(2)}) async-start(), calls=%async_computation.6 | async-start | bytes 983040 | tf_op jit(solution)/shard_map/reduce_scatter | solution.py:122
  198.2 13.5 %copy-start.3 = (bf16[384,2048]{1,0:T(8,128)(2,1)S(1)}, bf16[384,2048]{1,0:T(8,128)(2,1)}, u32[]{:S(2)}) copy-start(bf16[384,2048]{1,0:T(8,128)(2,1)} %get-tuple-element.9) | copy-start | bytes 4718596
  198.3 13.5 %copy-start.4 = (bf16[384,2048]{1,0:T(8,128)(2,1)S(1)}, bf16[384,2048]{1,0:T(8,128)(2,1)}, u32[]{:S(2)}) copy-start(bf16[384,2048]{1,0:T(8,128)(2,1)} %get-tuple-element.7) | copy-start | bytes 4718596
  198.3 13.5 %copy-start.9 = (bf16[384,3072]{1,0:T(8,128)(2,1)S(1)}, bf16[384,3072]{1,0:T(8,128)(2,1)}, u32[]{:S(2)}) copy-start(bf16[384,3072]{1,0:T(8,128)(2,1)} %all-gather.5.cloned.1.call-done) | copy-start | bytes 7077892
Sparse Core Ops, SparseCore 0:
  10.1 52.6 all-gather.4
  65.0 48.7 all-gather.2
  123.6 27.9 all-reduce.5
  195.9 45.8 reduce-scatter.5
  244.9 23.4 reduce-scatter.9
  271.1 26.3 reduce-scatter.7
where the time goes:
time: 356 us
  waiting for transfers between devices  131 us (37%)
  matrix products  105 us (29%)
  blocking collectives  91.1 us (26%)
  between operations  15.6 us (4%)
  local copies, waits for them, and re-layouts  7.8 us (2%)
  other arithmetic  4.83 us (1%)
    psum x1, blocking collectives, shards(): router_grad = lax.psum(router_part, ('dp', 'expert'))  76.5 us
    all_gather x1, waiting for transfers between devices, shards(): lax.all_gather(local_tokens, 'dp', axis=0, tiled=True)  50.6 us
    dot_general x3, matrix products, contract_cols(): lax.dot_general(left_side, right_side, (((1,), (1,)), ((), ())), preferre...  38 us
    dot_general x3, matrix products, contract_rows(): lax.dot_general(left_side, right_side, (((0,), (0,)), ((), ())), preferre...  36 us
    all_gather x1, waiting for transfers between devices, shards(): lax.all_gather(local_grads, 'dp', axis=0, tiled=True)  30.3 us
    psum x1, waiting for transfers between devices, shards(): lax.psum(grad_part.astype(jnp.bfloat16), 'tensor').astype(jnp.float32)  20 us
    reduce_scatter x1, waiting for transfers between devices, shards(): lax.psum_scatter(slot_dx.astype(jnp.bfloat16), 'dp', scatter_dimension=0,...  19.6 us
    unnamed x1, blocking collectives  12.1 us
  transfers between devices with their start and end apart: 6, of which 5 were waited for; matrix products, arithmetic and copies ran while one was open for 20% of the time, Pallas kernels for 0%

commit v1 on v0

--- a/solution.py
+++ b/solution.py
@@ -146,7 +146,7 @@
         jnp.bfloat16
     )
     router_part = jnp.dot(part_tokens.astype(jnp.float32).T, logit_grad, precision=highest)
-    router_grad = lax.psum(router_part, ("dp", "expert"))
+    router_grad = lax.psum(lax.psum(router_part, "expert"), "dp")
     return (tokens_grad, router_grad, gate_grad[None], up_grad[None], down_grad[None])
 
 

time: 356 us -> 316 us (0.89)
  blocking collectives: 91.1 us -> 50.6 us
    psum x1 -> x2, blocking collectives: 76.5 us -> 36 us  [shards(): router_grad = lax.psum(lax.psum(router_part, 'expert'), 'dp')]
  transfers between devices with their start and end apart: 6 -> 6, of which waited for: 5 -> 5; matrix products, arithmetic and copies ran while one was open for 20% -> 22% of each run, Pallas kernels for 0% -> 0%
where the time goes in v1:
time: 316 us; the launch traced here: 315 us
  waiting for transfers between devices  131 us (41%)
  matrix products  105 us (33%)
  blocking collectives  50.6 us (16%)
  between operations  15.6 us (5%)
  local copies, waits for them, and re-layouts  7.8 us (2%)
  other arithmetic  4.83 us (2%)
    all_gather x1, waiting for transfers between devices, shards(): lax.all_gather(local_tokens, 'dp', axis=0, tiled=True)  50.6 us
    dot_general x3, matrix products, contract_cols(): lax.dot_general(left_side, right_side, (((1,), (1,)), ((), ())), preferre...  38 us
    dot_general x3, matrix products, contract_rows(): lax.dot_general(left_side, right_side, (((0,), (0,)), ((), ())), preferre...  36 us
    psum x2, blocking collectives, shards(): router_grad = lax.psum(lax.psum(router_part, 'expert'), 'dp')  36 us
    all_gather x1, waiting for transfers between devices, shards(): lax.all_gather(local_grads, 'dp', axis=0, tiled=True)  30.2 us
    psum x1, waiting for transfers between devices, shards(): lax.psum(grad_part.astype(jnp.bfloat16), 'tensor').astype(jnp.float32)  20 us
    reduce_scatter x1, waiting for transfers between devices, shards(): lax.psum_scatter(slot_dx.astype(jnp.bfloat16), 'dp', scatter_dimension=0,...  19.6 us
    unnamed x1, blocking collectives  12.1 us
  transfers between devices with their start and end apart: 6, of which 5 were waited for; matrix products, arithmetic and copies ran while one was open for 22% of the time, Pallas kernels for 0%

profile of v1, /device:TPU:0, one launch (start us, length us, event | category | flops | bytes accessed | tf_op | source)
XLA Modules:
  0.0 315.4 jit_solution(14354826022559546774)
XLA Ops:
  7.2 0.8 slice_bitcast_fusion.1
  8.0 0.8 compare_bitcast_fusion.1
  8.8 1.1 convolution_convert_fusion
  10.0 2.3 convolution_convert_fusion.1
  12.3 50.6 %all-gather.5.cloned.1.call-done = bf16[384,3072]{1,0:T(8,128)(2,1)} async-done(((bf16[96,3072]{1,0:T(8,128)(2,1)}), bf16[384,3072]{1,0:T(8,128)(2,1)}) %all-gather.5.cloned.1.call-update) | async-done | bytes 2359312 | tf_op jit(solution)/shard_map/all_gather | solution.py:85
  62.9 11.3 %fusion.31 = bf16[384,2048]{1,0:T(8,128)(2,1)} fusion(bf16[384,3072]{1,0:T(8,128)(2,1)} %all-gather.5.cloned.1.call-done, bf16[1,3072,2048]{2,1,0:T(8,128)(2,1)} %param.11), kind=kOutput, calls=%fused_computation.44 | convolution fusion | flops 4832624640 | bytes 16515072 | tf_op jit(solution)/shard_map/dot_general | solution.py:92
  74.1 9.4 %fusion.28 = bf16[384,2048]{1,0:T(8,128)(2,1)} fusion(bf16[384,3072]{1,0:T(8,128)(2,1)S(1)} %copy-done.8, bf16[1,3072,2048]{2,1,0:T(8,128)(2,1)} %param.12), kind=kOutput, calls=%fused_computation.43 | convolution fusion | flops 4832624640 | bytes 16515072 | tf_op jit(solution)/shard_map/dot_general | solution.py:93
  83.5 30.2 %all-gather.3.cloned.1.call-done = bf16[384,3072]{1,0:T(8,128)(2,1)} async-done(((bf16[96,3072]{1,0:T(8,128)(2,1)}), bf16[384,3072]{1,0:T(8,128)(2,1)}) %all-gather.3.cloned.1.call-update) | async-done | bytes 2359312 | tf_op jit(solution)/shard_map/all_gather | solution.py:86
  113.8 9.6 %fusion.25 = bf16[384,2048]{1,0:T(8,128)(2,1)} fusion(bf16[384,3072]{1,0:T(8,128)(2,1)} %all-gather.3.cloned.1.call-done, bf16[1,2048,3072]{2,1,0:T(8,128)(2,1)} %param.13), kind=kOutput, calls=%fused_computation.42 | convolution fusion | flops 4832624640 | bytes 16515072 | tf_op jit(solution)/shard_map/dot_general | solution.py:17
  123.5 0.6 copy-done.6
  124.1 0.1 copy.59
  124.2 0.1 reshape.58
  124.4 0.3 fusion.66
  124.7 2.5 psum.42
  127.2 2.4 gather_fusion
  129.5 0.1 reshape.61
  129.7 0.6 fusion.65
  131.1 0.1 convolution_bitcast_fusion.3
  131.2 0.1 fusion.37
  131.3 0.2 dynamic-update-slice
  131.5 20.0 %all-reduce.6.cloned.1.call-done = (bf16[384,2048]{1,0:T(8,128)(2,1)}, bf16[384,2048]{1,0:T(8,128)(2,1)}, bf16[384,2048]{1,0:T(8,128)(2,1)}) async-done(((bf16[384,2048]{1,0:T(8,128)(2,1)}, bf16[384,2048]{1,0:T(8,128)(2,1)}, bf16[384,2048]{1,0:T(8,128)(2,1)}), (bf16[384,2048]{1,0:T(8,128)(2,1)}, bf16[384,2048]{1,0:T(8,128)(2,1)}, bf16[384,2048]{1,0:T(8,128)(2,1)})) %all-reduce.6.cloned.1.call-update) | async-done | bytes 4718608 | tf_op jit(solution)/shard_map/psum | solution.py:98
  151.5 3.7 %fusion.14 = bf16[384]{0:T(512)(128)(2,1)S(1)} fusion(bf16[384,2048]{1,0:T(8,128)(2,1)} %get-tuple-element.7, bf16[384,2048]{1,0:T(8,128)(2,1)} %get-tuple-element.8, bf16[384,2048]{1,0:T(8,128)(2,1)} %get-tuple-element.9), kind=kLoop, calls=%fused_computation.31 | loop fusion | flops 9436800 | bytes 4719360 | tf_op jit(solution)/shard_map/reduce_sum | solution.py:49
  155.2 12.1 %all-reduce.2 = (bf16[384]{0:T(512)(128)(2,1)S(1)}, bf16[384]{0:T(512)(128)(2,1)S(1)}) all-reduce(bf16[384]{0:T(512)(128)(2,1)S(1)} %fusion.14, bf16[384]{0:T(512)(128)(2,1)S(1)} %dynamic-update-slice), channel_id=4, replica_groups=mesh['dp'=4,'expert'=4,'tensor'=2] {'dp'}, use_global_device_ids=true, to_apply=%region_7.8.clone | all-reduce | flops 768 | bytes 3072
  167.4 12.2 %fusion = f32[384,3072]{1,0:T(8,128)} fusion(bf16[1,3072,2048]{2,1,0:T(8,128)(2,1)} %param.11, bf16[384,2048]{1,0:T(8,128)(2,1)S(1)} %copy-done.1, bf16[384,2048]{1,0:T(8,128)(2,1)} %get-tuple-element.7, bf16[384,2048]{1,0:T(8,128)(2,1)} %get-tuple-element.9, f32[384]{0:T(512)S(1)} %convert_element_type.124), kind=kOutput, calls=%fused_computation.2 | convolution fusion | flops 4842848256 | bytes 22021632 | tf_op jit(solution)/shard_map/dot_general | solution.py:17
  179.6 16.1 %add_convert_fusion = bf16[384,3072]{1,0:T(8,128)(2,1)} fusion(f32[384,3072]{1,0:T(8,128)} %fusion, bf16[1,3072,2048]{2,1,0:T(8,128)(2,1)} %param.12, bf16[384,2048]{1,0:T(8,128)(2,1)S(1)} %copy-done.2, bf16[384,2048]{1,0:T(8,128)(2,1)} %get-tuple-element.7, f32[384]{0:T(512)S(1)} %convert_element_type.124), kind=kOutput, calls=%fused_computation.20 | convolution fusion | flops 4841275392 | bytes 22808064 | tf_op jit(solution)/shard_map/dot_general | solution.py:17
  195.8 0.1 bitcast_or_fusion
  195.9 0.1 copy.61
  195.9 0.1 reshape.64
  196.7 0.2 convolution_bitcast_fusion.1
  196.9 0.2 fusion.35
  197.2 0.7 copy.63
  198.0 0.3 reduce-scatter.8.cloned.1.call-start
  198.3 13.5 %convert_bitcast_fusion.2 = bf16[1,3072,2048]{2,1,0:T(8,128)(2,1)} fusion(bf16[384,3072]{1,0:T(8,128)(2,1)} %all-gather.5.cloned.1.call-done, bf16[384,2048]{1,0:T(8,128)(2,1)S(1)} %copy-done.1, bf16[384,2048]{1,0:T(8,128)(2,1)} %get-tuple-element.7, bf16[384,2048]{1,0:T(8,128)(2,1)} %get-tuple-element.9, f32[384]{0:T(512)S(1)} %convert_element_type.124), kind=kOutput, calls=%fused_computation.14 | convolution fusion | flops 4849139712 | bytes 19662336 | tf_op jit(solution)/shard_map/dot_general | solution.py:11
  211.8 10.3 %convert_bitcast_fusion.1 = bf16[1,3072,2048]{2,1,0:T(8,128)(2,1)} fusion(bf16[384,3072]{1,0:T(8,128)(2,1)S(1)} %copy-done.9, bf16[384,2048]{1,0:T(8,128)(2,1)S(1)} %copy-done.3, bf16[384,2048]{1,0:T(8,128)(2,1)S(1)} %copy-done.4, f32[384]{0:T(512)S(1)} %convert_element_type.124), kind=kOutput, calls=%fused_computation.13 | convolution fusion | flops 4845207552 | bytes 18089472 | tf_op jit(solution)/shard_map/dot_general | solution.py:11
  222.1 19.6 %reduce-scatter.6.cloned.1.call-done = bf16[96,3072]{1,0:T(8,128)(2,1)} async-done(((bf16[384,3072]{1,0:T(8,128)(2,1)}), bf16[96,3072]{1,0:T(8,128)(2,1)}) %reduce-scatter.6.cloned.1.call-update) | async-done | bytes 589840 | tf_op jit(solution)/shard_map/reduce_scatter | solution.py:112
  241.7 1.5 fusion.48
  243.2 2.4 fusion.12
  245.6 12.1 %convert_bitcast_fusion = bf16[1,2048,3072]{2,1,0:T(8,128)(2,1)} fusion(bf16[384,3072]{1,0:T(8,128)(2,1)} %all-gather.3.cloned.1.call-done, f32[384]{0:T(512)S(1)} %convert_element_type.124, bf16[384,2048]{1,0:T(8,128)(2,1)S(1)} %copy-done.1, bf16[384,2048]{1,0:T(8,128)(2,1)} %get-tuple-element.9), kind=kOutput, calls=%fused_computation.12 | convolution fusion | flops 4847960064 | bytes 18089472 | tf_op jit(solution)/shard_map/dot_general | solution.py:11
  257.7 10.6 %reduce-scatter.10.cloned.1.call-done = bf16[32,4]{1,0:T(8,128)(2,1)} async-done(((bf16[128,4]{1,0:T(8,128)(2,1)}), bf16[32,4]{1,0:T(8,128)(2,1)}) %reduce-scatter.10.cloned.1.call-update) | async-done | bytes 272
  268.3 0.8 copy.64
  269.1 0.9 gather_fusion.1
  270.0 0.1 reshape.67
  270.1 0.1 copy.62
  270.2 0.1 multiply_reduce_fusion
  270.4 0.2 fusion.38
  270.6 15.9 %psum.46 = f32[3072,4]{0,1:T(4,128)S(1)} all-reduce(f32[3072,4]{0,1:T(4,128)S(1)} %fusion.38), channel_id=1, replica_groups=mesh['dp'=4,'expert'=4,'tensor'=2] {'expert'}, use_global_device_ids=true, to_apply=%region_11.12 | all-reduce | flops 12288 | bytes 98304 | tf_op jit(solution)/shard_map/psum | solution.py:149
  286.6 20.0 %psum.47 = f32[3072,4]{0,1:T(4,128)} all-reduce(f32[3072,4]{0,1:T(4,128)S(1)} %psum.46), channel_id=1, replica_groups=mesh['dp'=4,'expert'=4,'tensor'=2] {'dp'}, use_global_device_ids=true, to_apply=%region_12.13 | all-reduce | flops 12288 | bytes 98304 | tf_op jit(solution)/shard_map/psum | solution.py:149
  306.6 2.0 fusion.13
  (44 shorter events, 0.6 us)
Async XLA Ops:
  7.2 1.6 copy-start
  7.2 55.7 %all-gather.5.cloned.1.call-start = ((), (), s32[]{:S(2)}) async-start(), calls=%async_computation.4 | async-start | bytes 2949120 | tf_op jit(solution)/shard_map/all_gather | solution.py:85
  9.9 103.9 %all-gather.3.cloned.1.call-start = ((), (), s32[]{:S(2)}) async-start(), calls=%async_computation.3 | async-start | bytes 2949120 | tf_op jit(solution)/shard_map/all_gather | solution.py:86
  12.3 139.3 %all-reduce.6.cloned.1.call-start = ((), (), s32[]{:S(2)}) async-start(), calls=%async_computation.8 | async-start | bytes 9437184 | tf_op jit(solution)/shard_map/psum | solution.py:98
  62.9 11.3 %copy-start.8 = (bf16[384,3072]{1,0:T(8,128)(2,1)S(1)}, bf16[384,3072]{1,0:T(8,128)(2,1)}, u32[]{:S(2)}) copy-start(bf16[384,3072]{1,0:T(8,128)(2,1)} %all-gather.5.cloned.1.call-done) | copy-start | bytes 7077892
  123.4 0.7 copy-start.6
  123.4 0.9 copy-start.5
  123.5 118.3 %reduce-scatter.6.cloned.1.call-start = ((), (), s32[]{:S(2)}) async-start(), calls=%async_computation.5 | async-start | bytes 2949120 | tf_op jit(solution)/shard_map/reduce_scatter | solution.py:112
  127.2 2.6 copy-start.7
  151.5 15.8 %copy-start.1 = (bf16[384,2048]{1,0:T(8,128)(2,1)S(1)}, bf16[384,2048]{1,0:T(8,128)(2,1)}, u32[]{:S(2)}) copy-start(bf16[384,2048]{1,0:T(8,128)(2,1)} %get-tuple-element.8) | copy-start | bytes 4718596
  167.4 12.2 %copy-start.2 = (bf16[384,2048]{1,0:T(8,128)(2,1)S(1)}, bf16[384,2048]{1,0:T(8,128)(2,1)}, u32[]{:S(2)}) copy-start(bf16[384,2048]{1,0:T(8,128)(2,1)} %get-tuple-element.9) | copy-start | bytes 4718596
  195.7 72.6 %reduce-scatter.10.cloned.1.call-start = ((), (), s32[]{:S(2)}) async-start(), calls=%async_computation.7 | async-start | bytes 40960
  198.0 108.6 %reduce-scatter.8.cloned.1.call-start = ((), (), s32[]{:S(2)}) async-start(), calls=%async_computation.6 | async-start | bytes 983040 | tf_op jit(solution)/shard_map/reduce_scatter | solution.py:122
  198.2 13.5 %copy-start.3 = (bf16[384,2048]{1,0:T(8,128)(2,1)S(1)}, bf16[384,2048]{1,0:T(8,128)(2,1)}, u32[]{:S(2)}) copy-start(bf16[384,2048]{1,0:T(8,128)(2,1)} %get-tuple-element.9) | copy-start | bytes 4718596
  198.2 13.5 %copy-start.4 = (bf16[384,2048]{1,0:T(8,128)(2,1)S(1)}, bf16[384,2048]{1,0:T(8,128)(2,1)}, u32[]{:S(2)}) copy-start(bf16[384,2048]{1,0:T(8,128)(2,1)} %get-tuple-element.7) | copy-start | bytes 4718596
  198.2 13.5 %copy-start.9 = (bf16[384,3072]{1,0:T(8,128)(2,1)S(1)}, bf16[384,3072]{1,0:T(8,128)(2,1)}, u32[]{:S(2)}) copy-start(bf16[384,3072]{1,0:T(8,128)(2,1)} %all-gather.5.cloned.1.call-done) | copy-start | bytes 7077892
Sparse Core Ops, SparseCore 0:
  10.1 52.6 all-gather.4
  65.0 48.7 all-gather.2
  123.6 27.9 all-reduce.5
  195.8 45.8 reduce-scatter.5
  244.9 23.4 reduce-scatter.9
  271.1 26.2 reduce-scatter.7
